TPU v7x, 32 devices: a whole 2x2x4 slice. The times are simulated.
32 devices in a mesh: wide: 16 (over z, y, core), narrow: 2 (over x).
Axes of the slice: x: 2, y: 2, z: 4, core: 2. Of those that a mesh axis runs over, the one named last changes fastest.
Arguments:
- gradient: float32 [3072, 3072], P('wide', 'narrow'), may hold values from -6 to 6
- first_moment: float32 [3072, 3072], P('wide', 'narrow'), may hold values from -6 to 6
- second_moment: float32 [3072, 3072], P('wide', 'narrow'), may hold values from 0.25 to 4
- left_basis: float32 [3072, 3072], P('wide', 'narrow'), may hold values from -0.15625 to 0.15625
- right_basis: float32 [3072, 3072], P('wide', 'narrow'), may hold values from -0.109375 to 0.109375
Outputs:
- update: float32 [3072, 3072], P('wide', 'narrow')
- new_first: float32 [3072, 3072], P('wide', 'narrow')
- new_second: float32 [3072, 3072], P('wide', 'narrow')
All inputs are finite; a program needn't handle non-finite values.
Results may differ from a plain program's by a relative error of at most 0.000075.
Values sent between devices are 32-bit elements; how exact they have to be, the bound alone decides.
A program may use at most 128 MiB of HBM per device.

v0:
```python
import jax
import jax.numpy as jnp
from jax import lax
from jax.sharding import PartitionSpec as P

STEP = 10


beta_first = 0.9
beta_second = 0.95
epsilon = 1e-08


def product(left, right):
    return jnp.dot(left, right, precision=lax.Precision.HIGHEST, preferred_element_type=jnp.float32)


def contract(left, right, left_dim, right_dim):
    return lax.dot_general(
        left,
        right,
        (((left_dim,), (right_dim,)), ((), ())),
        precision=lax.Precision.HIGHEST,
        preferred_element_type=jnp.float32,
    )


def body(gradient, first_moment, second_moment, left_basis, right_basis):
    grad_rows, left_rows = (
        lax.all_gather(gradient, "narrow", axis=1, tiled=True),
        lax.all_gather(left_basis, "narrow", axis=1, tiled=True),
    )
    columns = grad_rows
    rotated_right = product(columns, lax.all_gather(right_basis, "wide", axis=0, tiled=True))
    columns = left_rows
    rotated = lax.psum_scatter(
        contract(columns, rotated_right, 0, 0), "wide", scatter_dimension=0, tiled=True
    )
    new_first = beta_first * first_moment + (1.0 - beta_first) * rotated
    new_second = beta_second * second_moment + (1.0 - beta_second) * rotated * rotated
    direction = (
        new_first
        / (1.0 - beta_first**STEP)
        / (jnp.sqrt(new_second / (1.0 - beta_second**STEP)) + epsilon)
    )
    columns = left_rows
    back_left = product(columns, lax.all_gather(direction, "wide", axis=0, tiled=True))
    terms = contract(back_left, lax.all_gather(right_basis, "wide", axis=0, tiled=True), 1, 1)
    update = lax.psum_scatter(terms, "narrow", scatter_dimension=1, tiled=True)
    return (update, new_first, new_second)


def solution(mesh):
    placed = (
        P("wide", "narrow"),
        P("wide", "narrow"),
        P("wide", "narrow"),
        P("wide", "narrow"),
        P("wide", "narrow"),
    )
    return jax.shard_map(
        body,
        mesh=mesh,
        in_specs=placed,
        out_specs=(P("wide", "narrow"), P("wide", "narrow"), P("wide", "narrow")),
        check_vma=False,
    )
```

profile of v0, /device:TPU:0, one launch (start us, length us, event | category | flops | bytes accessed | tf_op | source)
XLA Modules:
  0.0 637.2 jit_solution(4374816837675824320)
XLA Ops:
  7.2 0.0 all-gather.5.cloned.1.call-start
  7.2 0.7 all-gather.5.cloned.1.call-update
  7.9 0.0 all-gather.7.cloned.1.call-start
  7.9 0.7 all-gather.7.cloned.1.call-update
  8.6 0.0 all-gather.9.cloned.1.call-start
  8.7 0.7 all-gather.9.cloned.1.call-update
  9.4 0.0 reduce-scatter.7.cloned.1.call-start
  9.4 38.9 %all-gather.5.cloned.1.call-done = f32[192,3072]{1,0:T(8,128)} async-done(((f32[192,1536]{1,0:T(8,128)}), f32[192,3072]{1,0:T(8,128)}) %all-gather.5.cloned.1.call-update) | async-done | bytes 2359312 | tf_op jit(solution)/shard_map/all_gather | solution.py:30
  48.3 100.5 %all-gather.7.cloned.1.call-done = f32[3072,1536]{1,0:T(8,128)} async-done(((f32[192,1536]{1,0:T(8,128)}), f32[3072,1536]{1,0:T(8,128)}) %all-gather.7.cloned.1.call-update) | async-done | bytes 18874384 | tf_op jit(solution)/shard_map/all_gather | solution.py:34
  148.8 16.6 %fusion.2 = f32[192,1536]{1,0:T(8,128)S(1)} fusion(f32[192,3072]{1,0:T(8,128)} %all-gather.5.cloned.1.call-done, f32[3072,1536]{1,0:T(8,128)} %all-gather.7.cloned.1.call-done), kind=kOutput, calls=%fused_computation.5 | convolution fusion | flops 10871635968 | bytes 22413312 | tf_op jit(solution)/shard_map/dot_general | solution.py:15
  165.5 21.0 %all-gather.9.cloned.1.call-done = f32[192,3072]{1,0:T(8,128)} async-done(((f32[192,1536]{1,0:T(8,128)}), f32[192,3072]{1,0:T(8,128)}) %all-gather.9.cloned.1.call-update) | async-done | bytes 2359312 | tf_op jit(solution)/shard_map/all_gather | solution.py:31
  186.5 19.5 %convolution_bitcast_fusion = f32[3072,1536]{0,1:T(8,128)} fusion(f32[192,1536]{1,0:T(8,128)S(1)} %fusion.2, f32[192,3072]{1,0:T(8,128)} %all-gather.9.cloned.1.call-done), kind=kOutput, calls=%fused_computation | convolution fusion | flops 10871635968 | bytes 22413312 | tf_op jit(solution)/shard_map/dot_general | solution.py:19
  206.0 18.7 %copy.17 = f32[3072,1536]{1,0:T(8,128)} copy(f32[3072,1536]{0,1:T(8,128)} %convolution_bitcast_fusion) | data formatting | bytes 37748736
  224.7 0.0 copy-start.3
  224.7 0.0 reduce-scatter.7.cloned.1.call-update
  224.7 0.2 all-gather.11.cloned.1.call-start
  225.0 1.0 copy-done.3
  226.0 0.5 copy.12
  226.4 1.7 copy.13
  228.2 190.7 %reduce-scatter.7.cloned.1.call-done = f32[192,1536]{1,0:T(8,128)} async-done(((f32[3072,1536]{1,0:T(8,128)}), f32[192,1536]{1,0:T(8,128)}) %reduce-scatter.7.cloned.1.call-update) | async-done | bytes 1179664
  418.9 3.0 copy.18
  421.9 4.1 add_divide_fusion
  426.0 0.0 copy-start
  426.0 3.0 copy.14
  429.0 0.0 all-gather.11.cloned.1.call-update
  429.1 0.0 reduce-scatter.5.cloned.1.call-start
  429.1 98.1 %all-gather.11.cloned.1.call-done = f32[3072,1536]{1,0:T(8,128)} async-done(((f32[192,1536]{1,0:T(8,128)}), f32[3072,1536]{1,0:T(8,128)}) %all-gather.11.cloned.1.call-update) | async-done | bytes 18874384 | tf_op jit(solution)/shard_map/all_gather | solution.py:47
  527.2 0.0 copy-done
  527.2 32.5 %fusion.3 = f32[1536,192]{1,0:T(8,128)S(1)} fusion(f32[3072,1536]{1,0:T(8,128)} %all-gather.11.cloned.1.call-done, f32[192,3072]{1,0:T(8,128)S(1)} %copy-done), kind=kOutput, calls=%fused_computation.6 | convolution fusion | flops 10871635968 | bytes 22413312 | tf_op jit(solution)/shard_map/dot_general | solution.py:15
  559.8 35.7 %fusion.4 = f32[192,3072]{1,0:T(8,128)} fusion(f32[1536,192]{1,0:T(8,128)S(1)} %fusion.3, f32[3072,1536]{1,0:T(8,128)} %all-gather.7.cloned.1.call-done), kind=kOutput, calls=%fused_computation.7 | convolution fusion | flops 10871635968 | bytes 22413312 | tf_op jit(solution)/shard_map/dot_general | solution.py:19
  595.4 0.0 copy-start.2
  595.4 0.0 reduce-scatter.5.cloned.1.call-update
  595.5 0.0 copy-start.1
  595.5 1.4 copy-done.2
  596.8 1.5 copy.15
  598.3 0.0 copy-done.1
  598.3 1.5 copy.16
  599.8 30.6 %reduce-scatter.5.cloned.1.call-done = f32[192,1536]{1,0:T(8,128)} async-done(((f32[192,3072]{1,0:T(8,128)}), f32[192,1536]{1,0:T(8,128)}) %reduce-scatter.5.cloned.1.call-update) | async-done | bytes 1179664 | tf_op jit(solution)/shard_map/reduce_scatter | solution.py:49
Async XLA Ops:
  7.2 41.2 %all-gather.5.cloned.1.call-start = ((), (), s32[]{:S(2)}) async-start(), calls=%async_computation.2 | async-start | bytes 3538944 | tf_op jit(solution)/shard_map/all_gather | solution.py:30
  7.9 140.9 %all-gather.7.cloned.1.call-start = ((), (), s32[]{:S(2)}) async-start(), calls=%async_computation.3 | async-start | bytes 20054016 | tf_op jit(solution)/shard_map/all_gather | solution.py:34
  8.6 177.8 %all-gather.9.cloned.1.call-start = ((), (), s32[]{:S(2)}) async-start(), calls=%async_computation.4 | async-start | bytes 3538944 | tf_op jit(solution)/shard_map/all_gather | solution.py:31
  9.4 409.5 %reduce-scatter.7.cloned.1.call-start = ((), (), s32[]{:S(2)}) async-start(), calls=%async_computation.7 | async-start | bytes 20054016
  224.7 1.3 copy-start.3
  224.7 302.5 %all-gather.11.cloned.1.call-start = ((), (), s32[]{:S(2)}) async-start(), calls=%async_computation.5 | async-start | bytes 20054016 | tf_op jit(solution)/shard_map/all_gather | solution.py:47
  426.0 101.2 %copy-start = (f32[192,3072]{1,0:T(8,128)S(1)}, f32[192,3072]{1,0:T(8,128)}, u32[]{:S(2)}) copy-start(f32[192,3072]{1,0:T(8,128)} %all-gather.9.cloned.1.call-done) | copy-start | bytes 7077892
  429.1 201.3 %reduce-scatter.5.cloned.1.call-start = ((), (), s32[]{:S(2)}) async-start(), calls=%async_computation.6 | async-start | bytes 3538944 | tf_op jit(solution)/shard_map/reduce_scatter | solution.py:49
  595.4 1.4 copy-start.2
  595.5 2.9 copy-start.1
Sparse Core Ops, SparseCore 0:
  9.5 38.7 all-gather.4
  49.9 98.8 all-gather.6
  150.4 36.0 all-gather.8
  224.9 194.0 reduce-scatter.6
  429.2 98.0 all-gather.10
  595.6 34.7 reduce-scatter.4
where the time goes:
time: 638 us; the launch traced here: 637 us
  waiting for transfers between devices  482 us (76%)
  matrix products  104 us (16%)
  local copies, waits for them, and re-layouts  32.2 us (5%)
  between operations  14.2 us (2%)
    unnamed x7, waiting for transfers between devices  193 us
    all_gather x1, waiting for transfers between devices, body(): lax.all_gather(right_basis, 'wide', axis=0, tiled=True)  101 us
    all_gather x1, waiting for transfers between devices, body(): lax.all_gather(direction, 'wide', axis=0, tiled=True)  98.1 us
    dot_general x2, matrix products, contract(): lax.dot_general(left, right, (((left_dim,), (right_dim,)), ((), ())), pre...  55.2 us
    dot_general x2, matrix products, product(): jnp.dot(left, right, precision=lax.Precision.HIGHEST, preferred_element_t...  49.1 us
    all_gather x1, waiting for transfers between devices, body(): lax.all_gather(gradient, 'narrow', axis=1, tiled=True)  38.9 us
    reduce_scatter x1, waiting for transfers between devices, body(): update = lax.psum_scatter(terms, 'narrow', scatter_dimension=1, tiled=True)  30.6 us
    unnamed x14, local copies, waits for them, and re-layouts  29.2 us
  transfers between devices with their start and end apart: 6, of which 6 were waited for; matrix products, arithmetic and copies ran while one was open for 3% of the time, Pallas kernels for 0%

commit v1 on v0

v1 whole, which is shorter than its diff:
```python
import jax
import jax.numpy as jnp
from jax import lax
from jax.sharding import PartitionSpec as P

STEP = 10


beta_first = 0.9
beta_second = 0.95
epsilon = 1e-08


CHUNKS = 2


def contract(left, right, left_dim, right_dim):
    return lax.dot_general(
        left,
        right,
        (((left_dim,), (right_dim,)), ((), ())),
        precision=lax.Precision.HIGH,
        preferred_element_type=jnp.float32,
    )


def whole_rows(block):
    if lax.axis_size("narrow") != 2:
        return lax.all_gather(block, "narrow", axis=1, tiled=True)
    other = lax.ppermute(block, "narrow", ((0, 1), (1, 0)))
    first = lax.axis_index("narrow") == 0
    return jnp.concatenate(
        (jnp.where(first, block, other), jnp.where(first, other, block)), axis=1
    )


def body(gradient, first_moment, second_moment, left_basis, right_basis):
    width = gradient.shape[1] // CHUNKS
    parts = [slice(k * width, (k + 1) * width) for k in range(CHUNKS)]
    panel = lambda block: lax.all_gather(block, "wide", axis=0, tiled=True)

    left_rows = whole_rows(left_basis)
    grad_rows = whole_rows(gradient)
    left_columns = lax.all_to_all(left_rows, "wide", split_axis=1, concat_axis=0, tiled=True)

    rights = [panel(right_basis[:, part]) for part in parts]
    rotated_rights = [panel(contract(grad_rows, right, 1, 0)) for right in rights]
    firsts, seconds, terms = [], [], 0.0
    for part, right, rotated_right in zip(parts, rights, rotated_rights):
        rotated = contract(left_columns, rotated_right, 0, 0)
        new_first = beta_first * first_moment[:, part] + (1.0 - beta_first) * rotated
        new_second = beta_second * second_moment[:, part] + (1.0 - beta_second) * rotated * rotated
        direction = (
            new_first
            / (1.0 - beta_first**STEP)
            / (jnp.sqrt(new_second / (1.0 - beta_second**STEP)) + epsilon)
        )
        back_left = contract(left_rows, panel(direction), 1, 0)
        terms = terms + contract(back_left, right, 1, 1)
        firsts.append(new_first)
        seconds.append(new_second)
    update = lax.psum_scatter(terms, "narrow", scatter_dimension=1, tiled=True)
    return (update, jnp.concatenate(firsts, axis=1), jnp.concatenate(seconds, axis=1))


def solution(mesh):
    placed = (
        P("wide", "narrow"),
        P("wide", "narrow"),
        P("wide", "narrow"),
        P("wide", "narrow"),
        P("wide", "narrow"),
    )
    return jax.shard_map(
        body,
        mesh=mesh,
        in_specs=placed,
        out_specs=(P("wide", "narrow"), P("wide", "narrow"), P("wide", "narrow")),
        check_vma=False,
    )
```

time: 638 us -> 619 us (0.970)
  blocking collectives: 0 us -> 113 us
  waiting for transfers between devices: 482 us -> 404 us
  matrix products: 104 us -> 65 us
  local copies, waits for them, and re-layouts: 32.2 us -> 13.9 us
    unnamed x7, waiting for transfers between devices: 193 us -> 1.3 us
    all_to_all x0 -> x1, blocking collectives: none -> 113 us  [body(): lax.all_to_all(left_rows, 'wide', split_axis=1, concat_axis=0, tiled=True)]
    all_gather x4 -> x6, waiting for transfers between devices: 258 us -> 320 us  [body(): panel = lambda block: lax.all_gather(block, 'wide', axis=0, tiled=True)]
    ppermute x0 -> x2, waiting for transfers between devices: none -> 52.7 us  [whole_rows(): other = lax.ppermute(block, 'narrow', ((0, 1), (1, 0)))]
    dot_general x2 -> x0, matrix products: 49.1 us -> none  [product(): jnp.dot(left, right, precision=lax.Precision.HIGHEST, preferred_element_t...]
    unnamed x14 -> x18, local copies, waits for them, and re-layouts: 29.2 us -> 2.6 us
    dot_general x2 -> x8, matrix products: 55.2 us -> 65 us  [contract(): lax.dot_general(left, right, (((left_dim,), (right_dim,)), ((), ())), pre...]
    all_to_all x0 -> x2, local copies, waits for them, and re-layouts: none -> 6.55 us  [body(): lax.all_to_all(left_rows, 'wide', split_axis=1, concat_axis=0, tiled=True)]
  transfers between devices with their start and end apart: 6 -> 9, of which waited for: 6 -> 8; matrix products, arithmetic and copies ran while one was open for 3% -> 8% of each run, Pallas kernels for 0% -> 0%
where the time goes in v1:
time: 619 us
  waiting for transfers between devices  404 us (65%)
  blocking collectives  113 us (18%)
  matrix products  65 us (11%)
  between operations  14.2 us (2%)
  local copies, waits for them, and re-layouts  13.9 us (2%)
    all_gather x6, waiting for transfers between devices, body(): panel = lambda block: lax.all_gather(block, 'wide', axis=0, tiled=True)  320 us
    all_to_all x1, blocking collectives, body(): lax.all_to_all(left_rows, 'wide', split_axis=1, concat_axis=0, tiled=True)  113 us
    dot_general x8, matrix products, contract(): lax.dot_general(left, right, (((left_dim,), (right_dim,)), ((), ())), pre...  65 us
    ppermute x2, waiting for transfers between devices, whole_rows(): other = lax.ppermute(block, 'narrow', ((0, 1), (1, 0)))  52.7 us
    reduce_scatter x1, waiting for transfers between devices, body(): update = lax.psum_scatter(terms, 'narrow', scatter_dimension=1, tiled=True)  30.1 us
  transfers between devices with their start and end apart: 9, of which 8 were waited for; matrix products, arithmetic and copies ran while one was open for 8% of the time, Pallas kernels for 0%

profile of v1, /device:TPU:0, one launch (start us, length us, event | category | flops | bytes accessed | tf_op | source)
XLA Modules:
  0.0 618.7 jit_solution(15083365055625889020)
XLA Ops:
  7.2 0.0 all-gather.7.cloned.1.call-start
  7.2 2.4 fusion.10
  9.6 0.0 all-gather.7.cloned.1.call-update
  9.7 0.0 all-gather.13.cloned.1.call-start
  9.7 0.7 all-gather.13.cloned.1.call-update
  10.4 0.0 all-gather.9.cloned.1.call-start
  10.5 3.0 collective-permute-start.1
  13.5 26.1 %collective-permute-done.1 = f32[192,1536]{1,0:T(8,128)} collective-permute-done((f32[192,1536]{1,0:T(8,128)S(1)}, f32[192,1536]{1,0:T(8,128)}, u32[]{:S(2)}, u32[]{:S(2)}) %collective-permute-start.1) | collective-permute-done | bytes 1179680 | tf_op jit(solution)/shard_map/ppermute | solution.py:30
  39.6 1.4 broadcast_select_fusion.1
  41.0 53.5 %all-gather.7.cloned.1.call-done = f32[3072,768]{1,0:T(8,128)} async-done(((f32[192,768]{1,0:T(8,128)}), f32[3072,768]{1,0:T(8,128)}) %all-gather.7.cloned.1.call-update) | async-done | bytes 9437200 | tf_op jit(solution)/shard_map/all_gather | solution.py:40
  94.5 6.9 %fusion.1 = f32[192,768]{1,0:T(8,128)} fusion(f32[3072,768]{1,0:T(8,128)} %all-gather.7.cloned.1.call-done, f32[192,1536]{1,0:T(8,128)S(1)} %get-tuple-element.13, f32[192,1536]{1,0:T(8,128)S(1)} %get-tuple-element.12), kind=kOutput, calls=%fused_computation.4 | convolution fusion | flops 2718498816 | bytes 12386304 | tf_op jit(solution)/shard_map/dot_general | solution.py:18
  101.4 0.0 all-gather.9.cloned.1.call-update
  101.4 0.0 copy-start.8
  101.4 0.0 all-gather.15.cloned.1.call-start
  101.5 75.2 %all-gather.13.cloned.1.call-done = f32[3072,768]{1,0:T(8,128)} async-done(((f32[192,768]{1,0:T(8,128)}), f32[3072,768]{1,0:T(8,128)}) %all-gather.13.cloned.1.call-update) | async-done | bytes 9437200 | tf_op jit(solution)/shard_map/all_gather | solution.py:40
  176.7 6.9 %fusion = f32[192,768]{1,0:T(8,128)} fusion(f32[3072,768]{1,0:T(8,128)} %all-gather.13.cloned.1.call-done, f32[192,1536]{1,0:T(8,128)S(1)} %get-tuple-element.13, f32[192,1536]{1,0:T(8,128)S(1)} %get-tuple-element.12), kind=kOutput, calls=%fused_computation.3 | convolution fusion | flops 2718498816 | bytes 12386304 | tf_op jit(solution)/shard_map/dot_general | solution.py:18
  183.6 0.0 all-gather.15.cloned.1.call-update
  183.6 0.0 all-gather.11.cloned.1.call-start
  183.7 1.5 collective-permute-start
  185.2 26.7 %collective-permute-done = f32[192,1536]{1,0:T(8,128)S(1)} collective-permute-done((f32[192,1536]{1,0:T(8,128)S(1)}, f32[192,1536]{1,0:T(8,128)S(1)}, u32[]{:S(2)}, u32[]{:S(2)}) %collective-permute-start) | collective-permute-done | bytes 1179680 | tf_op jit(solution)/shard_map/ppermute | solution.py:30
  211.9 0.2 broadcast_select_fusion.3
  212.1 1.0 copy-done
  213.1 0.2 pad_maximum_fusion
  213.2 2.3 copy.9
  215.5 112.9 %all_to_all.19 = f32[192,16,192]{0,2,1:T(8,128)S(1)} all-to-all(f32[192,16,192]{0,2,1:T(8,128)} %bitcast.17), channel_id=1, replica_groups=mesh['wide'=16,'narrow'=2] {'wide'}, dimensions={1} | all-to-all | bytes 4718592 | tf_op jit(solution)/shard_map/all_to_all | solution.py:44
  328.5 3.4 copy.10
  331.9 3.1 all_to_all.17
  335.0 0.0 all-gather.9.cloned.1.call-done
  335.1 6.9 %fusion.11 = f32[192,768]{1,0:T(8,128)} fusion(f32[3072,192]{0,1:T(8,128)S(1)} %all_to_all.17, f32[3072,768]{1,0:T(8,128)} %all-gather.9.cloned.1.call-done), kind=kOutput, calls=%fused_computation.24 | convolution fusion | flops 2717908992 | bytes 12386304 | tf_op jit(solution)/shard_map/dot_general | solution.py:18
  341.9 48.6 %all-gather.15.cloned.1.call-done = f32[3072,768]{1,0:T(8,128)} async-done(((f32[192,768]{1,0:T(8,128)}), f32[3072,768]{1,0:T(8,128)}) %all-gather.15.cloned.1.call-update) | async-done | bytes 9437200 | tf_op jit(solution)/shard_map/all_gather | solution.py:40
  390.6 10.1 %add_divide_fusion = (f32[192,768]{1,0:T(8,128)}, f32[192,768]{1,0:T(8,128)}, f32[192,768]{1,0:T(8,128)}, f32[192,768]{1,0:T(8,128)}, f32[192,768]{1,0:T(8,128)}, /*index=5*/f32[192,768]{1,0:T(8,128)}) fusion(f32[192,1536]{1,0:T(8,128)} %param.6, f32[192,1536]{1,0:T(8,128)} %param.7, f32[192,768]{1,0:T(8,128)} %fusion.11, f32[3072,192]{0,1:T(8,128)S(1)} %all_to_all.17, ...), kind=kOutput, calls=%fused_computation.11 | convolution fusion | flops 2721153024 | bytes 18284544 | tf_op jit(solution)/shard_map/dot_general | solution.py:18
  400.7 0.0 all-gather.11.cloned.1.call-update
  400.7 0.0 all-gather.17.cloned.1.call-start
  400.7 0.5 all-gather.17.cloned.1.call-update
  401.3 0.3 reduce-scatter.2.cloned.1.call-start
  401.5 78.6 %all-gather.11.cloned.1.call-done = f32[3072,768]{1,0:T(8,128)} async-done(((f32[192,768]{1,0:T(8,128)}), f32[3072,768]{1,0:T(8,128)}) %all-gather.11.cloned.1.call-update) | async-done | bytes 9437200 | tf_op jit(solution)/shard_map/all_gather | solution.py:40
  480.2 7.5 %fusion.7 = f32[192,768]{1,0:T(8,128)S(1)} fusion(f32[3072,768]{1,0:T(8,128)} %all-gather.11.cloned.1.call-done, f32[192,1536]{1,0:T(8,128)} %copy-done, f32[192,1536]{1,0:T(8,128)S(1)} %get-tuple-element.14), kind=kOutput, calls=%fused_computation.22 | convolution fusion | flops 2718498816 | bytes 12386304 | tf_op jit(solution)/shard_map/dot_general | solution.py:18
  487.7 10.5 %fusion.12 = f32[192,3072]{1,0:T(8,128)} fusion(f32[192,768]{1,0:T(8,128)S(1)} %fusion.7, f32[3072,768]{1,0:T(8,128)} %all-gather.7.cloned.1.call-done), kind=kOutput, calls=%fused_computation.25 | convolution fusion | flops 2717908992 | bytes 12386304 | tf_op jit(solution)/shard_map/dot_general | solution.py:18
  498.2 64.0 %all-gather.17.cloned.1.call-done = f32[3072,768]{1,0:T(8,128)} async-done(((f32[192,768]{1,0:T(8,128)}), f32[3072,768]{1,0:T(8,128)}) %all-gather.17.cloned.1.call-update) | async-done | bytes 9437200 | tf_op jit(solution)/shard_map/all_gather | solution.py:40
  562.2 6.3 %fusion.6 = f32[192,768]{1,0:T(8,128)S(1)} fusion(f32[3072,768]{1,0:T(8,128)} %all-gather.17.cloned.1.call-done, f32[192,1536]{1,0:T(8,128)S(1)} %copy-done.1, f32[192,1536]{1,0:T(8,128)S(1)} %get-tuple-element.14), kind=kOutput, calls=%fused_computation.21 | convolution fusion | flops 2718498816 | bytes 12386304 | tf_op jit(solution)/shard_map/dot_general | solution.py:18
  568.6 9.9 %convolution_add_fusion = f32[192,3072]{1,0:T(8,128)} fusion(f32[192,3072]{1,0:T(8,128)S(1)} %copy-done.2, f32[192,768]{1,0:T(8,128)S(1)} %fusion.6, f32[3072,768]{1,0:T(8,128)} %all-gather.13.cloned.1.call-done), kind=kOutput, calls=%fused_computation | convolution fusion | flops 2718498816 | bytes 14745600 | tf_op jit(solution)/shard_map/dot_general | solution.py:18
  578.5 0.0 reduce-scatter.2.cloned.1.call-update
  578.5 1.0 copy-done.3
  579.5 0.2 copy-done.4
  579.7 0.2 copy-done.5
  579.9 0.2 copy-done.6
  580.1 1.7 pad_maximum_fusion.4
  581.8 30.1 %reduce-scatter.2.cloned.1.call-done = f32[192,1536]{1,0:T(8,128)} async-done(((f32[192,3072]{1,0:T(8,128)}), f32[192,1536]{1,0:T(8,128)}) %reduce-scatter.2.cloned.1.call-update) | async-done | bytes 1179664 | tf_op jit(solution)/shard_map/reduce_scatter | solution.py:62
  (12 shorter events, 0.0 us)
Async XLA Ops:
  7.2 3.3 copy-start.7
  7.2 87.3 %all-gather.7.cloned.1.call-start = ((), (), s32[]{:S(2)}) async-start(), calls=%async_computation.2 | async-start | bytes 10027008 | tf_op jit(solution)/shard_map/all_gather | solution.py:40
  9.7 167.0 %all-gather.13.cloned.1.call-start = ((), (), s32[]{:S(2)}) async-start(), calls=%async_computation.5 | async-start | bytes 10027008 | tf_op jit(solution)/shard_map/all_gather | solution.py:40
  10.4 324.6 %all-gather.9.cloned.1.call-start = ((), (), s32[]{:S(2)}) async-start(), calls=%async_computation.3 | async-start | bytes 10027008 | tf_op jit(solution)/shard_map/all_gather | solution.py:40
  10.5 29.1 %collective-permute-start.1 = (f32[192,1536]{1,0:T(8,128)S(1)}, f32[192,1536]{1,0:T(8,128)}, u32[]{:S(2)}, u32[]{:S(2)}) collective-permute-start(f32[192,1536]{1,0:T(8,128)S(1)} %copy-done.7), channel_id=1, source_target_pairs={{0,1},{1,0},{2,3},{3,2},{4,5},{5,4},{6,7},{7,6},{8,9},{9,8},{10,11... | collective-permute-start | bytes 3538952 | tf_op jit(solution)/shard_map/ppermute | solution.py:30
  101.4 82.3 %copy-start.8 = (f32[192,1536]{1,0:T(8,128)S(1)}, f32[192,1536]{1,0:T(8,128)}, u32[]{:S(2)}) copy-start(f32[192,1536]{1,0:T(8,128)} %param.8) | copy-start | bytes 3538948
  101.4 289.1 %all-gather.15.cloned.1.call-start = ((), (), s32[]{:S(2)}) async-start(), calls=%async_computation.6 | async-start | bytes 10027008 | tf_op jit(solution)/shard_map/all_gather | solution.py:40
  183.6 296.5 %all-gather.11.cloned.1.call-start = ((), (), s32[]{:S(2)}) async-start(), calls=%async_computation.4 | async-start | bytes 10027008 | tf_op jit(solution)/shard_map/all_gather | solution.py:40
  183.7 28.2 %collective-permute-start = (f32[192,1536]{1,0:T(8,128)S(1)}, f32[192,1536]{1,0:T(8,128)S(1)}, u32[]{:S(2)}, u32[]{:S(2)}) collective-permute-start(f32[192,1536]{1,0:T(8,128)S(1)} %copy-done.8), channel_id=1, source_target_pairs={{0,1},{1,0},{2,3},{3,2},{4,5},{5,4},{6,7},{7,6},{8,9},{9,8},{10,11... | collective-permute-start | bytes 3538952 | tf_op jit(solution)/shard_map/ppermute | solution.py:30
  212.0 1.0 copy-start
  400.7 161.5 %all-gather.17.cloned.1.call-start = ((), (), s32[]{:S(2)}) async-start(), calls=%async_computation.7 | async-start | bytes 10027008 | tf_op jit(solution)/shard_map/all_gather | solution.py:40
  401.3 210.6 %reduce-scatter.2.cloned.1.call-start = ((), (), s32[]{:S(2)}) async-start(), calls=%async_computation.8 | async-start | bytes 3538944 | tf_op jit(solution)/shard_map/reduce_scatter | solution.py:62
  487.7 74.5 %copy-start.1 = (f32[192,1536]{1,0:T(8,128)S(1)}, f32[192,1536]{1,0:T(8,128)}, u32[]{:S(2)}) copy-start(f32[192,1536]{1,0:T(8,128)} %copy-done) | copy-start | bytes 3538948
  562.2 6.3 %copy-start.2 = (f32[192,3072]{1,0:T(8,128)S(1)}, f32[192,3072]{1,0:T(8,128)}, u32[]{:S(2)}) copy-start(f32[192,3072]{1,0:T(8,128)} %fusion.12) | copy-start | bytes 7077892
  578.5 1.1 copy-start.3
  578.5 1.2 copy-start.4
  578.5 1.4 copy-start.5
  578.5 1.6 copy-start.6
Sparse Core Ops, SparseCore 0:
  10.8 83.6 all-gather.6
  97.3 79.3 all-gather.12
  179.6 123.6 all-gather.8
  306.0 84.5 all-gather.14
  400.8 79.3 all-gather.10
  482.9 79.3 all-gather.16
  578.6 33.1 reduce-scatter.1
